TPU v7x, 8 devices: a whole 2x2x1 slice. The times are simulated.
8 devices in a mesh: dp: 2 (over y, z), tp: 4 (over x, core).
Axes of the slice: x: 2, y: 2, z: 1, core: 2. Of those that a mesh axis runs over, the one named last changes fastest.
Arguments:
- x: bfloat16 [4096, 2048], P('dp'), parts along dimension 0
- w_gate: bfloat16 [2048, 8192], P(None, 'tp')
- w_up: bfloat16 [2048, 8192], P(None, 'tp')
- w_down: bfloat16 [8192, 2048], P('tp')
Outputs:
- output: bfloat16 [4096, 2048], P('dp'), parts along dimension 0
There are 2 independent parts. A program takes and returns all parts, laid end to end along the dimension named above; an argument that names none is the same for every part.
All inputs are finite; a program needn't handle non-finite values.
Results may differ from a plain program's by a relative error of at most 0.016.
Values are sent between devices in bfloat16 or wider.
A program may use at most 2 GiB of HBM per device.

v0:
```python
import jax
import jax.numpy as jnp
from jax import lax
from jax.sharding import PartitionSpec as P


def solution(mesh):
    def step(x, w_gate, w_up, w_down):
        gate = jnp.dot(x, w_gate, preferred_element_type=jnp.float32)
        up = jnp.dot(x, w_up, preferred_element_type=jnp.float32)
        hidden = (jax.nn.silu(gate) * up).astype(jnp.bfloat16)
        term = jnp.dot(hidden, w_down, preferred_element_type=jnp.float32).astype(jnp.bfloat16)
        return lax.psum(term, "tp")

    return jax.shard_map(
        step,
        mesh=mesh,
        in_specs=(P("dp", None), P(None, "tp"), P(None, "tp"), P("tp", None)),
        out_specs=P("dp", None),
        check_vma=False,
    )
```

profile of v0, /device:TPU:0, one launch (start us, length us, event | category | flops | bytes accessed | tf_op | source)
XLA Modules:
  0.0 242.7 jit_solution(9712414078601805179)
XLA Ops:
  6.5 0.0 all-reduce.2.cloned.1.call-start
  6.5 0.0 copy-start
  6.5 0.0 copy-start.1
  6.5 24.3 %fusion.1 = f32[2048,2048]{1,0:T(8,128)} fusion(bf16[2048,2048]{1,0:T(8,128)(2,1)} %param.4, bf16[2048,2048]{1,0:T(8,128)(2,1)} %param.5), kind=kOutput, calls=%fused_computation.3 | convolution fusion | flops 17179869184 | bytes 33554432 | tf_op jit(solution)/shard_map/dot_general | solution.py:9
  30.8 0.0 copy-done
  30.8 0.0 copy-done.1
  30.8 22.9 %multiply_convert_fusion.clone.4 = bf16[2048,2048]{1,0:T(8,128)(2,1)} fusion(f32[2048,2048]{1,0:T(8,128)} %fusion.1, bf16[2048,2048]{1,0:T(8,128)(2,1)S(1)} %copy-done, bf16[2048,2048]{1,0:T(8,128)(2,1)S(1)} %copy-done.1), kind=kOutput, calls=%fused_computation.clone.clone.clone.1 | convolution fusion | flops 17205035008 | bytes 41943040 | tf_op jit(solution)/shard_map/dot_general | solution.py:10
  53.7 23.6 %convolution_convert_fusion = bf16[2048,2048]{1,0:T(8,128)(2,1)} fusion(bf16[2048,2048]{1,0:T(8,128)(2,1)} %param.7, bf16[2048,2048]{1,0:T(8,128)(2,1)} %multiply_convert_fusion.clone.4), kind=kOutput, calls=%fused_computation.1 | convolution fusion | flops 17184063488 | bytes 25165824 | tf_op jit(solution)/shard_map/dot_general | solution.py:12
  77.3 0.0 all-reduce.2.cloned.1.call-update
  77.3 150.1 %all-reduce.2.cloned.1.call-done = bf16[2048,2048]{1,0:T(8,128)(2,1)} async-done(((bf16[2048,2048]{1,0:T(8,128)(2,1)}), bf16[2048,2048]{1,0:T(8,128)(2,1)}) %all-reduce.2.cloned.1.call-update) | async-done | bytes 8388624 | tf_op jit(solution)/shard_map/psum | solution.py:13
  227.4 8.4 %copy.6 = bf16[2048,2048]{1,0:T(8,128)(2,1)} copy(bf16[2048,2048]{1,0:T(8,128)(2,1)} %all-reduce.2.cloned.1.call-done) | data formatting | bytes 16777216
Async XLA Ops:
  6.5 220.9 %all-reduce.2.cloned.1.call-start = ((), (), s32[]{:S(2)}) async-start(), calls=%async_computation | async-start | bytes 16777216 | tf_op jit(solution)/shard_map/psum | solution.py:13
  6.5 24.3 %copy-start = (bf16[2048,2048]{1,0:T(8,128)(2,1)S(1)}, bf16[2048,2048]{1,0:T(8,128)(2,1)}, u32[]{:S(2)}) copy-start(bf16[2048,2048]{1,0:T(8,128)(2,1)} %param.4) | copy-start | bytes 25165828
  6.5 24.3 %copy-start.1 = (bf16[2048,2048]{1,0:T(8,128)(2,1)S(1)}, bf16[2048,2048]{1,0:T(8,128)(2,1)}, u32[]{:S(2)}) copy-start(bf16[2048,2048]{1,0:T(8,128)(2,1)} %param.6) | copy-start | bytes 25165828
Sparse Core Ops, SparseCore 0:
  77.4 149.9 all-reduce.1
where the time goes:
time: 243 us
  waiting for transfers between devices  150 us (62%)
  matrix products  70.7 us (29%)
  between operations  13.4 us (6%)
  local copies, waits for them, and re-layouts  8.45 us (3%)
    psum x1, waiting for transfers between devices, step(): return lax.psum(term, 'tp')  150 us
    dot_general x1, matrix products, step(): gate = jnp.dot(x, w_gate, preferred_element_type=jnp.float32)  24.3 us
    dot_general x1, matrix products, step(): jnp.dot(hidden, w_down, preferred_element_type=jnp.float32)  23.6 us
    dot_general x1, matrix products, step(): up = jnp.dot(x, w_up, preferred_element_type=jnp.float32)  22.9 us
    unnamed x5, local copies, waits for them, and re-layouts  8.45 us
  transfers between devices with their start and end apart: 1, of which 1 were waited for; matrix products, arithmetic and copies ran while one was open for 0% of the time, Pallas kernels for 0%

commit v1 on v0

v1 whole, which is shorter than its diff:
```python
import functools

import jax
import jax.numpy as jnp
from jax import lax
from jax.experimental import pallas as pl
from jax.experimental.pallas import tpu as pltpu
from jax.sharding import PartitionSpec as P

MESH = pl.DeviceIdType.MESH
BF16, F32 = jnp.bfloat16, jnp.float32
R = 256
C = 256


def kernel(
    n, x_hbm, wg_hbm, wu_hbm, wd_hbm, y, xb, wg, wu, wd, h, t_send, t_recv, rs_send, rs_recv, own,
    x_sem, w_sem, d_sem, ts_sem, tr_sem, rss_sem, rsr_sem, ags_sem, agr_sem, fs_sem, fr_sem, gs_sem, gr_sem,
):
    me = lax.axis_index("tp")
    a, c = me // 2, lax.rem(me, 2)
    sib = {"tp": me + 1 - 2 * c}
    across = {"tp": lax.rem(me + 2, 4)}
    tiles = wg.shape[0]

    def column(half, quarter, i):
        return pl.multiple_of(half * 4 * C + quarter * 2 * C + i * C, C)

    def at(ref, k, col):
        return ref.at[pl.ds(pl.multiple_of(k * R, R), R), pl.ds(col, C)]

    def down_column(u):
        half = 1 - c if u < 4 else c
        return column(half, 1 - a if u % 4 < 2 else a, u % 2)

    def load_x(k):
        return pltpu.make_async_copy(
            x_hbm.at[pl.ds(pl.multiple_of(k * R, R), R), :], xb.at[lax.rem(k, 2)], x_sem.at[lax.rem(k, 2)]
        )

    def load_w(j):
        cols = pl.ds(pl.multiple_of(j * C, C), C)
        return (
            pltpu.make_async_copy(wg_hbm.at[:, cols], wg.at[j], w_sem.at[0, j]),
            pltpu.make_async_copy(wu_hbm.at[:, cols], wu.at[j], w_sem.at[1, j]),
        )

    def load_d(u):
        return pltpu.make_async_copy(wd_hbm.at[:, pl.ds(down_column(u), C)], wd.at[u], d_sem.at[u])

    def remote(src, dst, ssem, rsem, to):
        return pltpu.make_async_remote_copy(src, dst, ssem, rsem, device_id=to, device_id_type=MESH)

    def term_copy(k, u):
        s = lax.rem(k, 2)
        return remote(t_send.at[s, u], t_recv.at[k, u], ts_sem.at[s, u], tr_sem.at[k, u], sib)

    def rs_copy(k, i):
        return remote(rs_send.at[k, i], rs_recv.at[k, i], rss_sem.at[k, i], rsr_sem.at[k, i], across)

    def ag_copy(k, i):
        part = at(y, k, column(c, a, i))
        return remote(part, part, ags_sem.at[k, i], agr_sem.at[k, i], across)

    def own_copy(k, i):
        part = at(y, k, column(c, a, i))
        return remote(part, part, fs_sem.at[k, i], fr_sem.at[k, i], sib)

    def pass_copy(k, i):
        part = at(y, k, column(c, 1 - a, i))
        return remote(part, part, gs_sem.at[k, i], gr_sem.at[k, i], sib)

    barrier = pltpu.get_barrier_semaphore()
    for to in (sib, across):
        pl.semaphore_signal(barrier, inc=1, device_id=to, device_id_type=MESH)

    load_x(0).start()
    for j in range(3):
        for copy in load_w(j):
            copy.start()

    def finish(k):
        for i in range(2):
            rs_copy(k, i).wait_recv()
            col = column(c, a, i)
            y[pl.ds(pl.multiple_of(k * R, R), R), pl.ds(col, C)] = (own[k, i] + rs_recv[k, i].astype(F32)).astype(BF16)
            ag_copy(k, i).start()
            own_copy(k, i).start()

    def chunk(k, first=False):
        slot = lax.rem(k, 2)

        @pl.when(k + 1 < n)
        def _():
            load_x(k + 1).start()

        load_x(k).wait()

        @pl.loop(0, tiles)
        def _(j):
            if first:
                @pl.when(j + 3 < tiles)
                def _():
                    for copy in load_w(j + 3):
                        copy.start()

                for s in range(3):
                    @pl.when(j == tiles - 3 + s)
                    def _():
                        for u in range(2 * s, 2 * s + 2 if s < 2 else 8):
                            load_d(u).start()

                for copy in load_w(j):
                    copy.wait()

            gate = jnp.dot(xb[slot], wg[j], preferred_element_type=F32)
            up = jnp.dot(xb[slot], wu[j], preferred_element_type=F32)
            h[:, pl.ds(pl.multiple_of(j * C, C), C)] = (jax.nn.silu(gate) * up).astype(BF16)

        if first:
            for u in range(8):
                load_d(u).wait()
            pl.semaphore_wait(barrier, 2)
        else:
            @pl.when(lax.rem(k, 3) != 2)
            def _():
                finish((2 * k + 1) // 3 - 1)

        @pl.loop(0, 4)
        def _(u):
            @pl.when(k >= 2)
            def _():
                term_copy(k, u).wait_send()

            t_send[slot, u] = jnp.dot(h[...], wd[u], preferred_element_type=F32).astype(BF16)
            term_copy(k, u).start()

        @pl.loop(0, 2)
        def _(i):
            term = jnp.dot(h[...], wd[4 + i], preferred_element_type=F32)
            term_copy(k, i).wait_recv()
            rs_send[k, i] = (term + t_recv[k, i].astype(F32)).astype(BF16)
            rs_copy(k, i).start()

        @pl.loop(0, 2)
        def _(i):
            term = jnp.dot(h[...], wd[6 + i], preferred_element_type=F32)
            term_copy(k, 2 + i).wait_recv()
            own[k, i] = term + t_recv[k, 2 + i].astype(F32)

    chunk(0, first=True)

    @pl.loop(1, n)
    def _(k):
        chunk(k)

    @pl.loop((2 * n - 1) // 3, n)
    def _(k):
        finish(k)

    @pl.loop(0, n)
    def _(k):
        for i in range(2):
            ag_copy(k, i).wait_recv()
            pass_copy(k, i).start()

    @pl.loop(0, n)
    def _(k):
        for i in range(2):
            own_copy(k, i).wait_recv()
            rs_copy(k, i).wait_send()
            ag_copy(k, i).wait_send()
            own_copy(k, i).wait_send()

    for s in range(2):
        for u in range(4):
            term_copy(s, u).wait_send()

    @pl.loop(0, n)
    def _(k):
        for i in range(2):
            pass_copy(k, i).wait()


def put_kernel(y_vmem, out, sem):
    copy = pltpu.make_async_copy(y_vmem, out, sem)
    copy.start()
    copy.wait()


def solution(mesh):
    def step(x, w_gate, w_up, w_down):
        rows, d = x.shape
        ff = w_gate.shape[1]
        n, tiles = rows // R, ff // C
        dma = pltpu.SemaphoreType.DMA
        y = pl.pallas_call(
            functools.partial(kernel, n),
            out_shape=pltpu.VMEM((rows, d), BF16),
            in_specs=[pl.BlockSpec(memory_space=pltpu.HBM)] * 4,
            out_specs=pl.BlockSpec(memory_space=pltpu.VMEM),
            scratch_shapes=[
                pltpu.VMEM((2, R, d), BF16),
                pltpu.VMEM((tiles, d, C), BF16),
                pltpu.VMEM((tiles, d, C), BF16),
                pltpu.VMEM((8, ff, C), BF16),
                pltpu.VMEM((R, ff), BF16),
                pltpu.VMEM((2, 4, R, C), BF16),
                pltpu.VMEM((n, 4, R, C), BF16),
                pltpu.VMEM((n, 2, R, C), BF16),
                pltpu.VMEM((n, 2, R, C), BF16),
                pltpu.VMEM((n, 2, R, C), F32),
                dma((2,)), dma((2, tiles)), dma((8,)),
                dma((2, 4)), dma((n, 4)), dma((n, 2)), dma((n, 2)), dma((n, 2)), dma((n, 2)),
                dma((n, 2)), dma((n, 2)), dma((n, 2)), dma((n, 2)),
            ],
            compiler_params=pltpu.CompilerParams(
                collective_id=0, has_side_effects=True, vmem_limit_bytes=52 * 2**20
            ),
            cost_estimate=pl.CostEstimate(
                flops=6 * rows * d * ff, bytes_accessed=2 * (2 * rows * d + 3 * d * ff), transcendentals=rows * ff
            ),
        )(x, w_gate, w_up, w_down)
        return y

    return jax.shard_map(
        step,
        mesh=mesh,
        in_specs=(P("dp", None), P(None, "tp"), P(None, "tp"), P("tp", None)),
        out_specs=P("dp", None),
        check_vma=False,
    )
```

time: 243 us -> 119 us (0.49)
  waiting for transfers between devices: 150 us -> 0 us
  Pallas kernels: 0 us -> 115 us
  matrix products: 70.7 us -> 0 us
  between operations: 13.4 us -> 0.01 us
  local copies, waits for them, and re-layouts: 8.45 us -> 3.4 us
    psum x1 -> x0, waiting for transfers between devices: 150 us -> none  [step(): return lax.psum(term, 'tp')]
    pallas_call x0 -> x1, Pallas kernels: none -> 115 us  [step(): pl.pallas_call(functools.partial(kernel, n), out_shape=pltpu.VMEM((rows,...]
    dot_general x3 -> x0, matrix products: 70.7 us -> none  [the longest x1 24.3 us: step(): gate = jnp.dot(x, w_gate, preferred_element_type=jnp.float32)]
    unnamed x5 -> x1, local copies, waits for them, and re-layouts: 8.45 us -> 3.4 us
  transfers between devices with their start and end apart: 1 -> 0, of which waited for: 1 -> 0; matrix products, arithmetic and copies ran while one was open for 0% -> 0% of each run, Pallas kernels for 0% -> 0%
where the time goes in v1:
time: 119 us
  Pallas kernels  115 us (97%)
  local copies, waits for them, and re-layouts  3.4 us (3%)
    pallas_call x1, Pallas kernels, step(): pl.pallas_call(functools.partial(kernel, n), out_shape=pltpu.VMEM((rows,...  115 us
    unnamed x1, local copies, waits for them, and re-layouts  3.4 us

profile of v1, /device:TPU:0, one launch (start us, length us, event | category | flops | bytes accessed | tf_op | source)
XLA Modules:
  0.0 118.9 jit_solution(8011703177469118333)
XLA Ops:
  0.0 115.5 %shard_map.46 = bf16[2048,2048]{1,0:T(8,128)(2,1)S(1)} custom-call(bf16[2048,2048]{1,0:T(8,128)(2,1)} %x_hbm.1, bf16[2048,2048]{1,0:T(8,128)(2,1)} %wg_hbm.1, bf16[2048,2048]{1,0:T(8,128)(2,1)} %wu_hbm.1, bf16[2048,2048]{1,0:T(8,128)(2,1)} %wd_hbm.1), custom_call_target="tpu_custom_call" | custom-call | flops 51539607552 | bytes 41943040 | tf_op jit(solution)/shard_map/pallas_call | solution.py:197
  115.5 3.4 %copy.6 = bf16[2048,2048]{1,0:T(8,128)(2,1)} copy(bf16[2048,2048]{1,0:T(8,128)(2,1)S(1)} %shard_map.46) | data formatting | bytes 16777216

commit v2 on v0

v2 whole, which is shorter than its diff:
```python
import functools

import jax
import jax.numpy as jnp
from jax import lax
from jax.experimental import pallas as pl
from jax.experimental.pallas import tpu as pltpu
from jax.sharding import PartitionSpec as P

MESH = pl.DeviceIdType.MESH
BF16, F32 = jnp.bfloat16, jnp.float32
R = 256
C = 256
AHEAD = 3
LAST = 2


def kernel(
    n, x_hbm, wg_hbm, wu_hbm, wd_hbm, y, xb, wgu, wd, h, t_send, t_recv, cross, rs_send, rs_recv, own,
    x_sem, w_sem, d_sem, ts_sem, tr_sem, ta_sem, rss_sem, rsr_sem, ags_sem, agr_sem, fs_sem, gs_sem, yr_sem,
):
    me = lax.axis_index("tp")
    a, c = me // 2, lax.rem(me, 2)
    sib = {"tp": me + 1 - 2 * c}
    across = {"tp": lax.rem(me + 2, 4)}
    tiles = wgu.shape[0]
    rows = n * R

    def column(half, quarter, i):
        return pl.multiple_of(half * 4 * C + quarter * 2 * C + i * C, C)

    def at(ref, k, col, chunks=1, wide=1):
        return ref.at[pl.ds(pl.multiple_of(k * R, R), chunks * R), pl.ds(col, wide * C)]

    def load_x(k):
        return pltpu.make_async_copy(
            x_hbm.at[pl.ds(pl.multiple_of(k * R, R), R), :], xb.at[lax.rem(k, 2)], x_sem.at[lax.rem(k, 2)]
        )

    def start_w(j):
        for m, w in enumerate((wg_hbm, wu_hbm)):
            pltpu.make_async_copy(w.at[:, pl.ds(j * C, C)], wgu.at[j, m], w_sem.at[j % AHEAD]).start(priority=1 if j else 0)

    def wait_w(j):
        pltpu.make_async_copy(wgu.at[j], wgu.at[j], w_sem.at[j % AHEAD]).wait()

    def load_d(u):
        half = 1 - c if u % 4 < 2 else c
        col = column(half, 1 - a if u < 4 else a, u % 2)
        return pltpu.make_async_copy(wd_hbm.at[:, pl.ds(col, C)], wd.at[u], d_sem.at[u // 4])

    def remote(src, dst, ssem, rsem, to):
        return pltpu.make_async_remote_copy(src, dst, ssem, rsem, device_id=to, device_id_type=MESH)

    def cross_term(k, i):
        return remote(t_send.at[k, i], t_recv.at[k, i], ts_sem, tr_sem.at[lax.rem(k, 4), i], sib)

    def own_term(k):
        two = pl.ds(2, 2)
        return remote(t_send.at[k, two], t_recv.at[k, two], ts_sem, ta_sem.at[lax.rem(k, 4)], sib)

    def rs_copy(k, i):
        return remote(rs_send.at[k, i], rs_recv.at[k, i], rss_sem, rsr_sem.at[lax.rem(k, 4), i], across)

    def ag_copy(k, i):
        part = at(y, k, column(c, a, i))
        slot = k // (n - LAST) * (1 + 2 * (k - (n - LAST)) + i)
        return remote(part, part, ags_sem, agr_sem.at[slot], across)

    def own_copy(k, i):
        part = at(y, k, column(c, a, i))
        return remote(part, part, fs_sem, yr_sem, sib)

    def pass_copy(k, i, chunks=1, wide=1):
        part = at(y, k, column(c, 1 - a, i), chunks, wide)
        return remote(part, part, gs_sem, yr_sem, sib)

    def drain(ref, sem):
        pltpu.make_async_copy(ref, ref, sem).wait()

    load_x(0).start()
    for j in range(AHEAD):
        start_w(j)
    barrier = pltpu.get_barrier_semaphore()
    for to in (sib, across):
        pl.semaphore_signal(barrier, inc=1, device_id=to, device_id_type=MESH)

    def down(u, first, count):
        return jnp.dot(h[pl.ds(first, count)], wd[u], preferred_element_type=F32)

    def down_two(us, put):
        parts = [down(u, 0, R) for u in us]
        for i, part in enumerate(parts):
            put(i, slice(None), part)

    def down_one(u, i, put):
        parts = [down(u, half * R // 2, R // 2) for half in range(2)]
        for half, part in enumerate(parts):
            put(i, pl.ds(half * R // 2, R // 2), part)

    def send_cross(k, i):
        cross_term(k, i).wait_recv()
        rs_send[k, i] = (cross[i] + t_recv[k, i].astype(F32)).astype(BF16)
        rs_copy(k, i).start()

    def finish(k, i):
        if i == 0:
            own_term(k).wait_recv()
        rs_copy(k, i).wait_recv()
        total = own[lax.rem(k, 2), i] + t_recv[k, 2 + i].astype(F32) + rs_recv[k, i].astype(F32)
        y[pl.ds(pl.multiple_of(k * R, R), R), pl.ds(column(c, a, i), C)] = total.astype(BF16)
        ag_copy(k, i).start()
        own_copy(k, i).start()

    def chunk(k, first=False):
        slot = lax.rem(k, 2)

        @pl.when(k + 1 < n)
        def _():
            load_x(k + 1).start()

        load_x(k).wait()
        groups = [[j] for j in range(tiles - 2)] + [[tiles - 2, tiles - 1]] if first else [range(tiles)]
        for g, group in enumerate(groups):
            if first:
                for j in group:
                    wait_w(j)
                for j in group:
                    if j + AHEAD < tiles:
                        start_w(j + AHEAD)
                if g >= len(groups) - 2:
                    for u in range(2) if g < len(groups) - 1 else range(2, 4):
                        load_d(u).start()
            for j in group:
                gate = jnp.dot(xb[slot], wgu[j, 0], preferred_element_type=F32)
                up = jnp.dot(xb[slot], wgu[j, 1], preferred_element_type=F32)
                h[:, pl.ds(j * C, C)] = (jax.nn.silu(gate) * up).astype(BF16)

        def put_send(i, part, value):
            t_send[k, i, part] = value.astype(BF16)

        def put_cross(i, part, value):
            cross[i, part] = value

        def put_later(i, part, value):
            t_send[k, 2 + i, part] = value.astype(BF16)

        def put_own(i, part, value):
            own[slot, i, part] = value

        if first:
            for u in range(4, 8):
                load_d(u).start()
            pl.semaphore_wait(barrier, 2)
            drain(wd.at[pl.ds(0, 4)], d_sem.at[0])
            for i in range(2):
                down_one(i, i, put_send)
                cross_term(k, i).start()
            for i in range(2):
                down_one(2 + i, i, put_cross)
                send_cross(k, i)
            drain(wd.at[pl.ds(4, 4)], d_sem.at[1])
        else:
            @pl.when(k == 1)
            def _():
                finish(0, 0)

            down_two((0, 1), put_send)
            for i in range(2):
                cross_term(k, i).start()
            down_two((2, 3), put_cross)
        down_two((4, 5), put_later)
        own_term(k).start()
        down_two((6, 7), put_own)

        if not first:
            for i in range(2):
                send_cross(k, i)

            @pl.when(k > 1)
            def _():
                finish(k - 1, 0)

            finish(k - 1, 1)

    chunk(0, first=True)

    @pl.loop(1, n)
    def _(k):
        chunk(k)

    for i in range(2):
        finish(n - 1, i)

    bulk = at(y, 0, column(c, 1 - a, 0), n - LAST, 2)
    drain(bulk, agr_sem.at[0])
    pass_copy(0, 0, n - LAST, 2).start()
    for k in range(n - LAST, n):
        for i in range(2):
            ag_copy(k, i).wait_recv()
            pass_copy(k, i).start()

    drain(t_send, ts_sem)
    drain(rs_send, rss_sem)
    mine = at(y, 0, column(c, a, 0), n, 2)
    drain(mine, ags_sem)
    drain(mine, fs_sem)
    drain(at(y, 0, column(c, 1 - a, 0), n, 2), gs_sem)
    drain(at(y, 0, column(1 - c, 0, 0), n, 4), yr_sem)


def solution(mesh):
    def step(x, w_gate, w_up, w_down):
        rows, d = x.shape
        ff = w_gate.shape[1]
        n, tiles = rows // R, ff // C
        dma = pltpu.SemaphoreType.DMA
        return pl.pallas_call(
            functools.partial(kernel, n),
            out_shape=pltpu.VMEM((rows, d), BF16),
            in_specs=[pl.BlockSpec(memory_space=pltpu.HBM)] * 4,
            out_specs=pl.BlockSpec(memory_space=pltpu.VMEM),
            scratch_shapes=[
                pltpu.VMEM((2, R, d), BF16),
                pltpu.VMEM((tiles, 2, d, C), BF16),
                pltpu.VMEM((8, ff, C), BF16),
                pltpu.VMEM((R, ff), BF16),
                pltpu.VMEM((n, 4, R, C), BF16),
                pltpu.VMEM((n, 4, R, C), BF16),
                pltpu.VMEM((2, R, C), F32),
                pltpu.VMEM((n, 2, R, C), BF16),
                pltpu.VMEM((n, 2, R, C), BF16),
                pltpu.VMEM((2, 2, R, C), F32),
                dma((2,)), dma((AHEAD,)), dma((2,)), dma(()), dma((4, 2)), dma((4,)), dma(()), dma((4, 2)),
                dma(()), dma((1 + 2 * LAST,)), dma(()), dma(()), dma(()),
            ],
            compiler_params=pltpu.CompilerParams(
                collective_id=0, has_side_effects=True, vmem_limit_bytes=52 * 2**20
            ),
            cost_estimate=pl.CostEstimate(
                flops=6 * rows * d * ff, bytes_accessed=2 * (2 * rows * d + 3 * d * ff), transcendentals=rows * ff
            ),
        )(x, w_gate, w_up, w_down)

    return jax.shard_map(
        step,
        mesh=mesh,
        in_specs=(P("dp", None), P(None, "tp"), P(None, "tp"), P("tp", None)),
        out_specs=P("dp", None),
        check_vma=False,
    )
```

time: 243 us -> 110 us (0.45)
  waiting for transfers between devices: 150 us -> 0 us
  Pallas kernels: 0 us -> 107 us
  matrix products: 70.7 us -> 0 us
  between operations: 13.4 us -> 0.01 us
  local copies, waits for them, and re-layouts: 8.45 us -> 3.4 us
    psum x1 -> x0, waiting for transfers between devices: 150 us -> none  [step(): return lax.psum(term, 'tp')]
    pallas_call x0 -> x1, Pallas kernels: none -> 107 us  [step(): pl.pallas_call(functools.partial(kernel, n), out_shape=pltpu.VMEM((rows,...]
    dot_general x3 -> x0, matrix products: 70.7 us -> none  [the longest x1 24.3 us: step(): gate = jnp.dot(x, w_gate, preferred_element_type=jnp.float32)]
    unnamed x5 -> x1, local copies, waits for them, and re-layouts: 8.45 us -> 3.4 us
  transfers between devices with their start and end apart: 1 -> 0, of which waited for: 1 -> 0; matrix products, arithmetic and copies ran while one was open for 0% -> 0% of each run, Pallas kernels for 0% -> 0%
where the time goes in v2:
time: 110 us
  Pallas kernels  107 us (97%)
  local copies, waits for them, and re-layouts  3.4 us (3%)
    pallas_call x1, Pallas kernels, step(): pl.pallas_call(functools.partial(kernel, n), out_shape=pltpu.VMEM((rows,...  107 us
    unnamed x1, local copies, waits for them, and re-layouts  3.4 us

profile of v2, /device:TPU:0, one launch (start us, length us, event | category | flops | bytes accessed | tf_op | source)
XLA Modules:
  0.0 110.1 jit_solution(2667965068401685760)
XLA Ops:
  0.0 106.7 %shard_map.46 = bf16[2048,2048]{1,0:T(8,128)(2,1)S(1)} custom-call(bf16[2048,2048]{1,0:T(8,128)(2,1)} %x_hbm.1, bf16[2048,2048]{1,0:T(8,128)(2,1)} %wg_hbm.1, bf16[2048,2048]{1,0:T(8,128)(2,1)} %wu_hbm.1, bf16[2048,2048]{1,0:T(8,128)(2,1)} %wd_hbm.1), custom_call_target="tpu_custom_call" | custom-call | flops 51539607552 | bytes 41943040 | tf_op jit(solution)/shard_map/pallas_call | solution.py:218
  106.7 3.4 %copy.6 = bf16[2048,2048]{1,0:T(8,128)(2,1)} copy(bf16[2048,2048]{1,0:T(8,128)(2,1)S(1)} %shard_map.46) | data formatting | bytes 16777216

commit v3 on v2

v3 whole, which is shorter than its diff:
```python
import functools

import jax
import jax.numpy as jnp
from jax import lax
from jax.experimental import pallas as pl
from jax.experimental.pallas import tpu as pltpu
from jax.sharding import PartitionSpec as P

MESH = pl.DeviceIdType.MESH
BF16, F32 = jnp.bfloat16, jnp.float32
R = 256
H = R // 2
C = 256
AHEAD = 3
LAST = 2


def kernel(
    n, x_hbm, wg_hbm, wu_hbm, wd_hbm, y, xb, wgu, wd, h, t_send, t_recv, cross, rs_send, rs_recv, own,
    x_sem, w_sem, d_sem, ts_sem, tr_sem, ta_sem, rss_sem, rsr_sem, ags_sem, agr_sem, fs_sem, gs_sem, yr_sem,
):
    me = lax.axis_index("tp")
    a, c = me // 2, lax.rem(me, 2)
    sib = {"tp": me + 1 - 2 * c}
    across = {"tp": lax.rem(me + 2, 4)}
    tiles = wgu.shape[0]
    rows = n * R

    def column(half, quarter, i):
        return pl.multiple_of(half * 4 * C + quarter * 2 * C + i * C, C)

    def span(half):
        return pl.ds(0, R) if half is None else pl.ds(half * H, H)

    def slot_of(k, half):
        return 4 if half == 1 else lax.rem(k, 4)

    def tile(k, i, half):
        first, count = (0, R) if half is None else (half * H, H)
        return pl.ds(pl.multiple_of(k * R + first, H), count), pl.ds(column(c, a, i), C)

    def at(ref, k, col, chunks=1, wide=1):
        return ref.at[pl.ds(pl.multiple_of(k * R, R), chunks * R), pl.ds(col, wide * C)]

    def load_x(k):
        return pltpu.make_async_copy(
            x_hbm.at[pl.ds(pl.multiple_of(k * R, R), R), :], xb.at[lax.rem(k, 2)], x_sem.at[lax.rem(k, 2)]
        )

    def start_w(j):
        for m, w in enumerate((wg_hbm, wu_hbm)):
            pltpu.make_async_copy(w.at[:, pl.ds(j * C, C)], wgu.at[j, m], w_sem.at[j % AHEAD]).start(priority=1 if j else 0)

    def wait_w(j):
        pltpu.make_async_copy(wgu.at[j], wgu.at[j], w_sem.at[j % AHEAD]).wait()

    def load_d(u):
        half = 1 - c if u % 4 < 2 else c
        col = column(half, 1 - a if u < 4 else a, u % 2)
        return pltpu.make_async_copy(wd_hbm.at[:, pl.ds(col, C)], wd.at[u], d_sem.at[u // 2])

    def remote(src, dst, ssem, rsem, to):
        return pltpu.make_async_remote_copy(src, dst, ssem, rsem, device_id=to, device_id_type=MESH)

    def cross_term(k, i, half):
        part = span(half)
        return remote(
            t_send.at[k, i, part], t_recv.at[k, i, part], ts_sem, tr_sem.at[slot_of(k, half), i], sib
        )

    def own_term(k, half):
        two, part = pl.ds(2, 2), span(half)
        return remote(
            t_send.at[k, two, part], t_recv.at[k, two, part], ts_sem, ta_sem.at[slot_of(k, half)], sib
        )

    def rs_copy(k, i, half):
        part = span(half)
        return remote(
            rs_send.at[k, i, part], rs_recv.at[k, i, part], rss_sem, rsr_sem.at[slot_of(k, half), i], across
        )

    def ag_copy(k, i, half=None):
        part = y.at[tile(k, i, half)]
        slot = k // (n - LAST) * (1 + 2 * (k - (n - LAST)) + i)
        return remote(part, part, ags_sem, agr_sem.at[slot], across)

    def own_copy(k, i, half):
        part = y.at[tile(k, i, half)]
        return remote(part, part, fs_sem, yr_sem, sib)

    def pass_copy(k, i, chunks=1, wide=1):
        part = at(y, k, column(c, 1 - a, i), chunks, wide)
        return remote(part, part, gs_sem, yr_sem, sib)

    def drain(ref, sem):
        pltpu.make_async_copy(ref, ref, sem).wait()

    load_x(0).start()
    for j in range(AHEAD):
        start_w(j)
    barrier = pltpu.get_barrier_semaphore()
    for to in (sib, across):
        pl.semaphore_signal(barrier, inc=1, device_id=to, device_id_type=MESH)

    def send_cross(k, i, half=None):
        part = span(half)
        cross_term(k, i, half).wait_recv()
        rs_send[k, i, part] = (cross[i, part] + t_recv[k, i, part].astype(F32)).astype(BF16)
        rs_copy(k, i, half).start()

    def finish(k, i, half=None):
        part = span(half)
        if i == 0:
            own_term(k, half).wait_recv()
        rs_copy(k, i, half).wait_recv()
        total = own[lax.rem(k, 2), i, part] + t_recv[k, 2 + i, part].astype(F32) + rs_recv[k, i, part].astype(F32)
        y[tile(k, i, half)] = total.astype(BF16)
        ag_copy(k, i, half).start()
        own_copy(k, i, half).start()

    def hidden(k, j, half):
        slot, part = lax.rem(k, 2), span(half)
        rows = xb[slot, part]
        gate = jnp.dot(rows, wgu[j, 0], preferred_element_type=F32)
        up = jnp.dot(rows, wgu[j, 1], preferred_element_type=F32)
        h[part, pl.ds(j * C, C)] = (jax.nn.silu(gate) * up).astype(BF16)

    def down(pair, half):
        rows = h[span(half)]
        return [jnp.dot(rows, wd[2 * pair + i], preferred_element_type=F32) for i in range(2)]

    def down_cross_send(k, half=None):
        for i, term in enumerate(down(0, half)):
            t_send[k, i, span(half)] = term.astype(BF16)
        for i in range(2):
            cross_term(k, i, half).start()

    def down_cross(half=None):
        for i, term in enumerate(down(1, half)):
            cross[i, span(half)] = term

    def down_own_send(k, half=None):
        for i, term in enumerate(down(2, half)):
            t_send[k, 2 + i, span(half)] = term.astype(BF16)
        own_term(k, half).start()

    def down_own(k, half=None):
        for i, term in enumerate(down(3, half)):
            own[lax.rem(k, 2), i, span(half)] = term

    def wait_d(pair):
        drain(wd.at[pl.ds(2 * pair, 2)], d_sem.at[pair])

    load_x(0).wait()
    for j in range(tiles):
        wait_w(j)
        if j + AHEAD < tiles:
            start_w(j + AHEAD)
        else:
            for u in range(2 * (j + AHEAD - tiles), 2 * (j + AHEAD - tiles) + 2):
                load_d(u).start()
        hidden(0, j, 0)
    pl.semaphore_wait(barrier, 2)
    for u in range(2 * AHEAD, 8):
        load_d(u).start()
    load_x(1).start()
    wait_d(0)
    down_cross_send(0, 0)
    wait_d(1)
    down_cross(0)
    for i in range(2):
        send_cross(0, i, 0)
    wait_d(2)
    down_own_send(0, 0)
    wait_d(3)
    down_own(0, 0)

    for j in range(tiles):
        hidden(0, j, 1)
    finish(0, 0, 0)
    down_cross_send(0, 1)
    down_cross(1)
    down_own_send(0, 1)
    for i in range(2):
        send_cross(0, i, 1)
    down_own(0, 1)
    finish(0, 1, 0)

    @pl.loop(1, n)
    def _(k):
        @pl.when(k + 1 < n)
        def _():
            load_x(k + 1).start()

        load_x(k).wait()
        for j in range(tiles):
            hidden(k, j, None)

        @pl.when(k == 1)
        def _():
            for i in range(2):
                finish(0, i, 1)

        @pl.when(k == 2)
        def _():
            finish(1, 0)

        down_cross_send(k)
        down_cross()
        down_own_send(k)
        down_own(k)
        for i in range(2):
            send_cross(k, i)

        @pl.when(k > 2)
        def _():
            finish(k - 1, 0)

        @pl.when(k > 1)
        def _():
            finish(k - 1, 1)

    for i in range(2):
        finish(n - 1, i)

    bulk = at(y, 0, column(c, 1 - a, 0), n - LAST, 2)
    drain(bulk, agr_sem.at[0])
    pass_copy(0, 0, n - LAST, 2).start()
    for k in range(n - LAST, n):
        for i in range(2):
            ag_copy(k, i).wait_recv()
            pass_copy(k, i).start()

    drain(t_send, ts_sem)
    drain(rs_send, rss_sem)
    mine = at(y, 0, column(c, a, 0), n, 2)
    drain(mine, ags_sem)
    drain(mine, fs_sem)
    drain(at(y, 0, column(c, 1 - a, 0), n, 2), gs_sem)
    drain(at(y, 0, column(1 - c, 0, 0), n, 4), yr_sem)


def solution(mesh):
    def step(x, w_gate, w_up, w_down):
        rows, d = x.shape
        ff = w_gate.shape[1]
        n, tiles = rows // R, ff // C
        dma = pltpu.SemaphoreType.DMA
        return pl.pallas_call(
            functools.partial(kernel, n),
            out_shape=pltpu.VMEM((rows, d), BF16),
            in_specs=[pl.BlockSpec(memory_space=pltpu.HBM)] * 4,
            out_specs=pl.BlockSpec(memory_space=pltpu.VMEM),
            scratch_shapes=[
                pltpu.VMEM((2, R, d), BF16),
                pltpu.VMEM((tiles, 2, d, C), BF16),
                pltpu.VMEM((8, ff, C), BF16),
                pltpu.VMEM((R, ff), BF16),
                pltpu.VMEM((n, 4, R, C), BF16),
                pltpu.VMEM((n, 4, R, C), BF16),
                pltpu.VMEM((2, R, C), F32),
                pltpu.VMEM((n, 2, R, C), BF16),
                pltpu.VMEM((n, 2, R, C), BF16),
                pltpu.VMEM((2, 2, R, C), F32),
                dma((2,)), dma((AHEAD,)), dma((4,)), dma(()), dma((5, 2)), dma((5,)), dma(()), dma((5, 2)),
                dma(()), dma((1 + 2 * LAST,)), dma(()), dma(()), dma(()),
            ],
            compiler_params=pltpu.CompilerParams(
                collective_id=0, has_side_effects=True, vmem_limit_bytes=52 * 2**20
            ),
            cost_estimate=pl.CostEstimate(
                flops=6 * rows * d * ff, bytes_accessed=2 * (2 * rows * d + 3 * d * ff), transcendentals=rows * ff
            ),
        )(x, w_gate, w_up, w_down)

    return jax.shard_map(
        step,
        mesh=mesh,
        in_specs=(P("dp", None), P(None, "tp"), P(None, "tp"), P("tp", None)),
        out_specs=P("dp", None),
        check_vma=False,
    )
```

time: 110 us -> 109 us (level)
  no operation moved by 1% of the time
where the time goes in v3:
time: 109 us
  Pallas kernels  106 us (97%)
  local copies, waits for them, and re-layouts  3.4 us (3%)
    pallas_call x1, Pallas kernels, step(): pl.pallas_call(functools.partial(kernel, n), out_shape=pltpu.VMEM((rows,...  106 us
    unnamed x1, local copies, waits for them, and re-layouts  3.4 us

profile of v3, /device:TPU:0, one launch (start us, length us, event | category | flops | bytes accessed | tf_op | source)
XLA Modules:
  0.0 109.3 jit_solution(3755842368118410327)
XLA Ops:
  0.0 105.9 %shard_map.46 = bf16[2048,2048]{1,0:T(8,128)(2,1)S(1)} custom-call(bf16[2048,2048]{1,0:T(8,128)(2,1)} %x_hbm.1, bf16[2048,2048]{1,0:T(8,128)(2,1)} %wg_hbm.1, bf16[2048,2048]{1,0:T(8,128)(2,1)} %wu_hbm.1, bf16[2048,2048]{1,0:T(8,128)(2,1)} %wd_hbm.1), custom_call_target="tpu_custom_call" | custom-call | flops 51539607552 | bytes 41943040 | tf_op jit(solution)/shard_map/pallas_call | solution.py:251
  105.9 3.4 %copy.6 = bf16[2048,2048]{1,0:T(8,128)(2,1)} copy(bf16[2048,2048]{1,0:T(8,128)(2,1)S(1)} %shard_map.46) | data formatting | bytes 16777216

commit v4 on v3

--- a/solution.py
+++ b/solution.py
@@ -112,8 +112,8 @@
 
     def finish(k, i, half=None):
         part = span(half)
-        if i == 0:
-            own_term(k, half).wait_recv()
+        if i == 0 and half != 1:
+            own_term(k, None).wait_recv()
         rs_copy(k, i, half).wait_recv()
         total = own[lax.rem(k, 2), i, part] + t_recv[k, 2 + i, part].astype(F32) + rs_recv[k, i, part].astype(F32)
         y[tile(k, i, half)] = total.astype(BF16)
@@ -172,21 +172,19 @@
     down_cross(0)
     for i in range(2):
         send_cross(0, i, 0)
-    wait_d(2)
-    down_own_send(0, 0)
-    wait_d(3)
-    down_own(0, 0)
 
     for j in range(tiles):
         hidden(0, j, 1)
-    finish(0, 0, 0)
     down_cross_send(0, 1)
     down_cross(1)
-    down_own_send(0, 1)
+    wait_d(2)
+    down_own_send(0)
     for i in range(2):
         send_cross(0, i, 1)
-    down_own(0, 1)
-    finish(0, 1, 0)
+    wait_d(3)
+    down_own(0)
+    for i in range(2):
+        finish(0, i, 0)
 
     @pl.loop(1, n)
     def _(k):

time: 109 us -> 109 us (level)
  no operation moved by 1% of the time
where the time goes in v4:
time: 109 us
  Pallas kernels  105 us (96%)
  local copies, waits for them, and re-layouts  3.4 us (3%)
    pallas_call x1, Pallas kernels, step(): pl.pallas_call(functools.partial(kernel, n), out_shape=pltpu.VMEM((rows,...  105 us
    unnamed x1, local copies, waits for them, and re-layouts  3.4 us

profile of v4, /device:TPU:0, one launch (start us, length us, event | category | flops | bytes accessed | tf_op | source)
XLA Modules:
  0.0 108.9 jit_solution(11275352992964341797)
XLA Ops:
  0.0 105.5 %shard_map.46 = bf16[2048,2048]{1,0:T(8,128)(2,1)S(1)} custom-call(bf16[2048,2048]{1,0:T(8,128)(2,1)} %x_hbm.1, bf16[2048,2048]{1,0:T(8,128)(2,1)} %wg_hbm.1, bf16[2048,2048]{1,0:T(8,128)(2,1)} %wu_hbm.1, bf16[2048,2048]{1,0:T(8,128)(2,1)} %wd_hbm.1), custom_call_target="tpu_custom_call" | custom-call | flops 51539607552 | bytes 41943040 | tf_op jit(solution)/shard_map/pallas_call | solution.py:249
  105.5 3.4 %copy.6 = bf16[2048,2048]{1,0:T(8,128)(2,1)} copy(bf16[2048,2048]{1,0:T(8,128)(2,1)S(1)} %shard_map.46) | data formatting | bytes 16777216
